TPU v7x, 32 devices: a whole 2x2x4 slice. The times are simulated.
32 devices in a mesh: dp: 8 (over z, y), mp: 4 (over x, core).
Axes of the slice: x: 2, y: 2, z: 4, core: 2. Of those that a mesh axis runs over, the one named last changes fastest.
Arguments:
- queries: bfloat16 [1024, 8192], P('dp', 'mp'), may hold values from -8 to 8
- tree_keys: bfloat16 [1024, 1024], P('dp', 'mp'), may hold values from -18 to 18
- tree_values: bfloat16 [1024, 1024], P('dp', 'mp'), may hold values from -6 to 6
- cache_keys: bfloat16 [16, 4096, 1024], P('dp', None, 'mp'), may hold values from -8 to 8
- cache_values: bfloat16 [16, 4096, 1024], P('dp', None, 'mp'), may hold values from -6 to 6
- cache_lens: int32 [16], P('dp'), may hold values from 1024 to 4096, as said below
- parents: int32 [16, 64], P('dp'), may hold values from -1 to 62, as said below
- accepted_nodes: int32 [16, 8], P('dp'), may hold values from 0 to 63, as said below
- residual: bfloat16 [1024, 8192], P('dp', 'mp'), may hold values from -1.796875 to 1.796875
- out_weight: bfloat16 [8192, 8192], P('mp', 'dp'), may hold values from -0.0625 to 0.0625
Outputs:
- tree_hidden: bfloat16 [1024, 8192], P('dp', 'mp')
- accepted_hidden: bfloat16 [128, 8192], P(None, 'mp')
Inputs may be any that keep to these rules, and one draw needn't show every extreme that they name: parents[r, 0] = -1 and 0 <= parents[r, i] < i for i >= 1. accepted_nodes[r, 0] = 0, the nodes of a row increase, and parents[r, accepted_nodes[r, a + 1]] = accepted_nodes[r, a]. `cache_lens`: some request has exactly 4096 filled positions.
All inputs are finite; a program needn't handle non-finite values.
Results may differ from a plain program's by a relative error of at most 0.015.
Values may be sent and summed in bfloat16 or wider, within the bound.
A program may use at most 64 MiB of HBM per device.

v0:
```python
import math
import jax
import jax.numpy as jnp
from jax import lax
from jax.sharding import PartitionSpec as P

HEADS = 64
KV_HEADS = 8
HD = 128
neg_large = -1e30


def ancestry(parents, node_count):
    positions = jnp.arange(node_count, dtype=jnp.int32)
    parent_hot = (parents[:, :, None] == positions[None, None, :]).astype(jnp.float32)
    reached = parent_hot + jnp.eye(node_count, dtype=jnp.float32)[None]
    for squaring in range((node_count - 1).bit_length()):
        reached = jnp.minimum(
            jnp.einsum("rij,rjk->rik", reached, reached, precision=lax.Precision.HIGHEST), 1.0
        )
    return reached > 0.5


def per_device(
    queries,
    tree_keys,
    tree_values,
    cache_keys,
    cache_values,
    cache_lens,
    parents,
    accepted_nodes,
    residual,
    out_weight,
):
    request_count = parents.shape[0]
    node_count = parents.shape[1]
    cache_length = cache_keys.shape[1]
    kv_local = tree_keys.shape[1] // HD
    group_size = HEADS // KV_HEADS
    scale_factor = 1.0 / math.sqrt(HD)
    query_grid = queries.reshape(request_count, node_count, kv_local, group_size, HD)
    tree_key_grid = tree_keys.reshape(request_count, node_count, kv_local, HD)
    tree_value_grid = tree_values.reshape(request_count, node_count, kv_local, HD)
    cache_key_grid = cache_keys.reshape(request_count, cache_length, kv_local, HD)
    cache_value_grid = cache_values.reshape(request_count, cache_length, kv_local, HD)
    ancestor = ancestry(parents, node_count)
    tree_scores = (
        jnp.einsum(
            "rnkgd,rjkd->rnkgj", query_grid, tree_key_grid, preferred_element_type=jnp.float32
        )
        * scale_factor
    )
    tree_scores = jnp.where(ancestor[:, :, None, None, :], tree_scores, neg_large)
    run_max = jnp.max(tree_scores, axis=-1)
    tree_weights = jnp.exp(tree_scores - run_max[..., None])
    run_sum = jnp.sum(tree_weights, axis=-1)
    run_acc = jnp.einsum(
        "rnkgj,rjkd->rnkgd",
        tree_weights.astype(jnp.bfloat16),
        tree_value_grid,
        preferred_element_type=jnp.float32,
    )
    block_len = min(512, cache_length)

    def absorb(block_number, state_now):
        old_max, old_sum, old_acc = state_now
        block_start = block_number * block_len
        key_block = lax.dynamic_slice_in_dim(cache_key_grid, block_start, block_len, 1)
        value_block = lax.dynamic_slice_in_dim(cache_value_grid, block_start, block_len, 1)
        block_scores = (
            jnp.einsum(
                "rnkgd,rpkd->rnkgp", query_grid, key_block, preferred_element_type=jnp.float32
            )
            * scale_factor
        )
        positions = block_start + jnp.arange(block_len, dtype=jnp.int32)
        live_keys = positions[None, :] < cache_lens[:, None]
        block_scores = jnp.where(live_keys[:, None, None, None, :], block_scores, neg_large)
        new_max = jnp.maximum(old_max, jnp.max(block_scores, axis=-1))
        block_weights = jnp.exp(block_scores - new_max[..., None])
        rescale = jnp.exp(old_max - new_max)
        new_sum = old_sum * rescale + jnp.sum(block_weights, axis=-1)
        new_acc = old_acc * rescale[..., None] + jnp.einsum(
            "rnkgp,rpkd->rnkgd",
            block_weights.astype(jnp.bfloat16),
            value_block,
            preferred_element_type=jnp.float32,
        )
        return (new_max, new_sum, new_acc)

    trip_count = cache_length // block_len
    run_max, run_sum, run_acc = lax.fori_loop(0, trip_count, absorb, (run_max, run_sum, run_acc))
    attended = (run_acc / run_sum[..., None]).astype(jnp.bfloat16)
    attended = attended.reshape(request_count * node_count, kv_local * group_size * HD)
    feature_share = residual.shape[1]
    all_rows = jnp.dot(
        lax.all_gather(attended, "dp", axis=0, tiled=True),
        out_weight,
        preferred_element_type=jnp.float32,
    )
    partial_sum = lax.all_to_all(
        all_rows.astype(jnp.bfloat16), "dp", split_axis=0, concat_axis=1, tiled=True
    ).astype(all_rows.dtype)
    head_total_sum = lax.psum(partial_sum.astype(jnp.bfloat16), "mp").astype(jnp.float32)
    own_share = lax.dynamic_slice_in_dim(
        head_total_sum, lax.axis_index("mp") * feature_share, feature_share, 1
    )
    tree_hidden = (residual.astype(jnp.float32) + own_share).astype(jnp.bfloat16)
    row_base = jnp.arange(request_count, dtype=jnp.int32)[:, None] * node_count
    picked_rows = (row_base + accepted_nodes).reshape(-1)
    picked_hidden = jnp.take(tree_hidden, picked_rows, axis=0)
    accepted_hidden = lax.all_gather(picked_hidden, "dp", axis=0, tiled=True)
    return (tree_hidden, accepted_hidden)


def solution(mesh):
    placed = (
        P("dp", "mp"),
        P("dp", "mp"),
        P("dp", "mp"),
        P("dp", None, "mp"),
        P("dp", None, "mp"),
        P("dp"),
        P("dp", None),
        P("dp", None),
        P("dp", "mp"),
        P("mp", "dp"),
    )
    return jax.shard_map(
        per_device,
        mesh=mesh,
        in_specs=placed,
        out_specs=(P("dp", "mp"), P(None, "mp")),
        check_vma=False,
    )
```

profile of v0, /device:TPU:0, one launch (start us, length us, event | category | flops | bytes accessed | tf_op | source)
XLA Modules:
  0.0 305.0 jit_solution(8466349382810361783)
XLA Ops:
  13.3 6.4 %copy.23 = bf16[2,4096,256]{1,2,0:T(8,128)(2,1)} copy(bf16[2,4096,256]{2,1,0:T(8,128)(2,1)} %param.15) | data formatting | bytes 8388608 | tf_op args[3]
  19.7 6.4 %copy.24 = bf16[2,4096,256]{1,2,0:T(8,128)(2,1)} copy(bf16[2,4096,256]{2,1,0:T(8,128)(2,1)} %param.16) | data formatting | bytes 8388608 | tf_op args[4]
  26.1 49.3 %while.17 = (s32[]{:T(128)}, f32[2,64,2,8]{1,3,2,0:T(8,128)S(1)}, f32[2,64,2,8]{1,3,2,0:T(8,128)S(1)}, f32[2,64,2,8,128]{4,1,3,2,0:T(8,128)S(1)}, s32[2]{0:T(128...) while((s32[]{:T(128)}, f32[2,64,2,8]{1,3,2,0:T(8,128)S(1)}, ...), condition=%wide.region_5.6_spmd, body=%wide.region_2.5_spmd.sunk | while | flops 548935168 | bytes 16392375 | solution.py:93
  26.2 1.8 bitcast_reduce_fusion.2
  29.7 2.5 fusion.62
  32.3 1.8 bitcast_reduce_fusion.2
  35.9 2.5 fusion.62
  38.5 1.8 bitcast_reduce_fusion.2
  42.1 2.5 fusion.62
  44.7 1.8 bitcast_reduce_fusion.2
  48.2 2.5 fusion.62
  50.8 1.8 bitcast_reduce_fusion.2
  54.4 2.5 fusion.62
  57.0 1.8 bitcast_reduce_fusion.2
  60.6 2.5 fusion.62
  63.2 1.8 bitcast_reduce_fusion.2
  66.7 2.5 fusion.62
  69.3 1.8 bitcast_reduce_fusion.2
  72.9 2.5 fusion.62
  77.2 75.6 %all-gather.2.cloned.1.call-done = bf16[1024,2048]{1,0:T(8,128)(2,1)} async-done(((bf16[128,2048]{1,0:T(8,128)(2,1)}), bf16[1024,2048]{1,0:T(8,128)(2,1)}) %all-gather.2.cloned.1.call-update) | async-done | bytes 4194320 | tf_op jit(solution)/shard_map/all_gather | solution.py:98
  152.8 7.9 %convolution_convert_fusion = bf16[1024,1024]{1,0:T(8,128)(2,1)S(1)} fusion(bf16[1024,2048]{1,0:T(8,128)(2,1)} %all-gather.2.cloned.1.call-done, bf16[2048,1024]{1,0:T(8,128)(2,1)} %param.21), kind=kOutput, calls=%fused_computation.27 | convolution fusion | flops 4296015872 | bytes 10485760 | tf_op jit(solution)/shard_map/dot_general | solution.py:97
  160.8 51.1 %all_to_all.19 = bf16[8,128,1024]{2,1,0:T(8,128)(2,1)S(1)} all-to-all(bf16[8,128,1024]{2,1,0:T(8,128)(2,1)S(1)} %bitcast.87), channel_id=1, replica_groups=mesh['dp'=8,'mp'=4] {'dp'}, dimensions={0} | all-to-all | bytes 4194304 | tf_op jit(solution)/shard_map/all_to_all | solution.py:102
  213.7 50.2 %all-reduce.2.cloned.1.call-done = bf16[128,8192]{1,0:T(8,128)(2,1)} async-done(((bf16[128,8192]{1,0:T(8,128)(2,1)}), bf16[128,8192]{1,0:T(8,128)(2,1)}) %all-reduce.2.cloned.1.call-update) | async-done | bytes 2097168 | tf_op jit(solution)/shard_map/psum | solution.py:105
  265.7 31.6 %all_gather.7 = bf16[128,2048]{1,0:T(8,128)(2,1)S(1)} all-gather(bf16[16,2048]{1,0:T(8,128)(2,1)S(1)} %broadcast_select_fusion), channel_id=1, replica_groups=mesh['dp'=8,'mp'=4] {'dp'}, dimensions={0}, use_global_device_ids=true | all-gather | bytes 589824 | tf_op jit(solution)/shard_map/all_gather | solution.py:113
  (94 shorter events, 26.6 us)
Async XLA Ops:
  7.2 5.6 %copy-start.2 = (bf16[128,256]{1,0:T(8,128)(2,1)S(1)}, bf16[128,256]{1,0:T(8,128)(2,1)}, u32[]{:S(2)}) copy-start(bf16[128,256]{1,0:T(8,128)(2,1)} %param.14) | copy-start | bytes 196612
  7.2 145.7 %all-gather.2.cloned.1.call-start = ((), (), s32[]{:S(2)}) async-start(), calls=%async_computation.1 | async-start | bytes 4718592 | tf_op jit(solution)/shard_map/all_gather | solution.py:98
  19.7 6.4 %copy-start.3 = (s32[2]{0:T(128)S(1)}, s32[2]{0:T(128)}, u32[]{:S(2)}) copy-start(s32[2]{0:T(128)} %param.17) | copy-start | bytes 28
  77.2 186.7 %all-reduce.2.cloned.1.call-start = ((), (), s32[]{:S(2)}) async-start(), calls=%async_computation.2 | async-start | bytes 4194304 | tf_op jit(solution)/shard_map/psum | solution.py:105
  211.9 1.5 copy-start.4
  211.9 51.9 %copy-start.1 = (bf16[128,2048]{1,0:T(8,128)(2,1)S(1)}, bf16[128,2048]{1,0:T(8,128)(2,1)}, u32[]{:S(2)}) copy-start(bf16[128,2048]{1,0:T(8,128)(2,1)} %param.20) | copy-start | bytes 1572868
  265.1 33.1 %copy-start = (bf16[128,2048]{1,0:T(8,128)(2,1)}, bf16[128,2048]{1,0:T(8,128)(2,1)S(1)}, u32[]{:S(2)}) copy-start(bf16[128,2048]{1,0:T(8,128)(2,1)S(1)} %add_convert_fusion) | copy-start | bytes 1572868
Sparse Core Ops, SparseCore 0:
  77.3 75.5 all-gather.1
  213.5 50.2 all-reduce.1
where the time goes:
time: 306 us; the launch traced here: 305 us
  waiting for transfers between devices  126 us (41%)
  blocking collectives  82.7 us (27%)
  matrix products  45.3 us (15%)
  local copies, waits for them, and re-layouts  20 us (7%)
  other arithmetic  16.3 us (5%)
  between operations  14.2 us (5%)
    all_gather x1, waiting for transfers between devices, per_device(): lax.all_gather(attended, 'dp', axis=0, tiled=True)  75.6 us
    all_to_all x1, blocking collectives, per_device(): lax.all_to_all(all_rows.astype(jnp.bfloat16), 'dp', split_axis=0, concat_...  51.1 us
    psum x1, waiting for transfers between devices, per_device(): lax.psum(partial_sum.astype(jnp.bfloat16), 'mp').astype(jnp.float32)  50.2 us
    all_gather x1, blocking collectives, per_device(): accepted_hidden = lax.all_gather(picked_hidden, 'dp', axis=0, tiled=True)  31.6 us
    dot_general x8, matrix products, absorb(): jnp.einsum('rnkgp,rpkd->rnkgd', block_weights.astype(jnp.bfloat16), value...  19.8 us
    unnamed x14, local copies, waits for them, and re-layouts  14.7 us
    dot_general x8, matrix products, absorb(): jnp.einsum('rnkgd,rpkd->rnkgp', query_grid, key_block, preferred_element_...  14.7 us
    reduce_sum x8, other arithmetic, absorb(): new_sum = old_sum * rescale + jnp.sum(block_weights, axis=-1)  13.6 us
  transfers between devices with their start and end apart: 2, of which 2 were waited for; matrix products, arithmetic and copies ran while one was open for 0% of the time, Pallas kernels for 0%

commit v1 on v0

--- a/solution.py
+++ b/solution.py
@@ -110,7 +110,12 @@
     row_base = jnp.arange(request_count, dtype=jnp.int32)[:, None] * node_count
     picked_rows = (row_base + accepted_nodes).reshape(-1)
     picked_hidden = jnp.take(tree_hidden, picked_rows, axis=0)
-    accepted_hidden = lax.all_gather(picked_hidden, "dp", axis=0, tiled=True)
+    ring = [picked_hidden]
+    for hop in range(7):
+        ring.append(lax.ppermute(ring[-1], "dp", [(dev, (dev + 1) % 8) for dev in range(8)]))
+    accepted_hidden = jnp.roll(
+        jnp.concatenate(ring[::-1], axis=0), (lax.axis_index("dp") + 1) * ring[0].shape[0], axis=0
+    )
     return (tree_hidden, accepted_hidden)
 
 

time: 306 us -> 324 us (1.059)
  waiting for transfers between devices: 126 us -> 174 us
  blocking collectives: 82.7 us -> 51.1 us
    ppermute x0 -> x7, waiting for transfers between devices: none -> 47.8 us  [per_device(): lax.ppermute(ring[-1], 'dp', [(dev, (dev + 1) % 8) for dev in range(8)])]
    all_gather x1 -> x0, blocking collectives: 31.6 us -> none  [per_device(): accepted_hidden = lax.all_gather(picked_hidden, 'dp', axis=0, tiled=True)]
    unnamed x14 -> x27, local copies, waits for them, and re-layouts: 14.7 us -> 14.2 us
  transfers between devices with their start and end apart: 2 -> 9, of which waited for: 2 -> 9; matrix products, arithmetic and copies ran while one was open for 0% -> 0% of each run, Pallas kernels for 0% -> 0%
where the time goes in v1:
time: 324 us; the launch traced here: 323 us
  waiting for transfers between devices  174 us (54%)
  blocking collectives  51.1 us (16%)
  matrix products  45.3 us (14%)
  local copies, waits for them, and re-layouts  20.3 us (6%)
  other arithmetic  16.5 us (5%)
  between operations  14.3 us (4%)
    all_gather x1, waiting for transfers between devices, per_device(): lax.all_gather(attended, 'dp', axis=0, tiled=True)  75.6 us
    all_to_all x1, blocking collectives, per_device(): lax.all_to_all(all_rows.astype(jnp.bfloat16), 'dp', split_axis=0, concat_...  51.1 us
    psum x1, waiting for transfers between devices, per_device(): lax.psum(partial_sum.astype(jnp.bfloat16), 'mp').astype(jnp.float32)  50.2 us
    ppermute x7, waiting for transfers between devices, per_device(): lax.ppermute(ring[-1], 'dp', [(dev, (dev + 1) % 8) for dev in range(8)])  47.8 us
    dot_general x8, matrix products, absorb(): jnp.einsum('rnkgp,rpkd->rnkgd', block_weights.astype(jnp.bfloat16), value...  19.8 us
    dot_general x8, matrix products, absorb(): jnp.einsum('rnkgd,rpkd->rnkgp', query_grid, key_block, preferred_element_...  14.6 us
    unnamed x27, local copies, waits for them, and re-layouts  14.2 us
    reduce_sum x8, other arithmetic, absorb(): new_sum = old_sum * rescale + jnp.sum(block_weights, axis=-1)  13.6 us
  transfers between devices with their start and end apart: 9, of which 9 were waited for; matrix products, arithmetic and copies ran while one was open for 0% of the time, Pallas kernels for 0%

profile of v1, /device:TPU:0, one launch (start us, length us, event | category | flops | bytes accessed | tf_op | source)
XLA Modules:
  0.0 323.2 jit_solution(9475230920322701339)
XLA Ops:
  13.3 6.4 %copy.23 = bf16[2,4096,256]{1,2,0:T(8,128)(2,1)} copy(bf16[2,4096,256]{2,1,0:T(8,128)(2,1)} %param.15) | data formatting | bytes 8388608 | tf_op args[3]
  19.7 6.5 %copy.24 = bf16[2,4096,256]{1,2,0:T(8,128)(2,1)} copy(bf16[2,4096,256]{2,1,0:T(8,128)(2,1)} %param.16) | data formatting | bytes 8388608 | tf_op args[4]
  26.2 49.3 %while.17 = (s32[]{:T(128)}, f32[2,64,2,8]{1,3,2,0:T(8,128)S(1)}, f32[2,64,2,8]{1,3,2,0:T(8,128)S(1)}, f32[2,64,2,8,128]{4,1,3,2,0:T(8,128)S(1)}, s32[2]{0:T(128...) while((s32[]{:T(128)}, f32[2,64,2,8]{1,3,2,0:T(8,128)S(1)}, ...), condition=%wide.region_5.6_spmd, body=%wide.region_2.5_spmd.sunk | while | flops 548935168 | bytes 16392375 | solution.py:93
  29.9 2.5 fusion.62
  36.0 2.5 fusion.62
  38.6 1.8 bitcast_reduce_fusion.2
  42.2 2.5 fusion.62
  48.4 2.5 fusion.62
  54.6 2.5 fusion.62
  60.7 2.5 fusion.62
  63.3 1.8 bitcast_reduce_fusion.2
  66.9 2.5 fusion.62
  73.1 2.5 fusion.62
  77.3 75.6 %all-gather.2.cloned.1.call-done = bf16[1024,2048]{1,0:T(8,128)(2,1)} async-done(((bf16[128,2048]{1,0:T(8,128)(2,1)}), bf16[1024,2048]{1,0:T(8,128)(2,1)}) %all-gather.2.cloned.1.call-update) | async-done | bytes 4194320 | tf_op jit(solution)/shard_map/all_gather | solution.py:98
  153.0 7.9 %convolution_convert_fusion = bf16[1024,1024]{1,0:T(8,128)(2,1)S(1)} fusion(bf16[1024,2048]{1,0:T(8,128)(2,1)} %all-gather.2.cloned.1.call-done, bf16[2048,1024]{1,0:T(8,128)(2,1)} %param.21), kind=kOutput, calls=%fused_computation.27 | convolution fusion | flops 4296015872 | bytes 10485760 | tf_op jit(solution)/shard_map/dot_general | solution.py:97
  160.9 51.1 %all_to_all.19 = bf16[8,128,1024]{2,1,0:T(8,128)(2,1)S(1)} all-to-all(bf16[8,128,1024]{2,1,0:T(8,128)(2,1)S(1)} %bitcast.87), channel_id=1, replica_groups=mesh['dp'=8,'mp'=4] {'dp'}, dimensions={0} | all-to-all | bytes 4194304 | tf_op jit(solution)/shard_map/all_to_all | solution.py:102
  213.9 50.2 %all-reduce.2.cloned.1.call-done = bf16[128,8192]{1,0:T(8,128)(2,1)} async-done(((bf16[128,8192]{1,0:T(8,128)(2,1)}), bf16[128,8192]{1,0:T(8,128)(2,1)}) %all-reduce.2.cloned.1.call-update) | async-done | bytes 2097168 | tf_op jit(solution)/shard_map/psum | solution.py:105
  267.4 5.5 %collective-permute-done = bf16[16,2048]{1,0:T(8,128)(2,1)S(1)} collective-permute-done((bf16[16,2048]{1,0:T(8,128)(2,1)S(1)}, bf16[16,2048]{1,0:T(8,128)(2,1)S(1)}, u32[]{:S(2)}, u32[]{:S(2)}) %collective-permute-start) | collective-permute-done | bytes 65568 | tf_op jit(solution)/shard_map/ppermute | solution.py:115
  272.8 7.0 %collective-permute-done.1 = bf16[16,2048]{1,0:T(8,128)(2,1)S(1)} collective-permute-done((bf16[16,2048]{1,0:T(8,128)(2,1)S(1)}, bf16[16,2048]{1,0:T(8,128)(2,1)S(1)}, u32[]{:S(2)}, u32[]{:S(2)}) %collective-permute-start.1) | collective-permute-done | bytes 65568 | tf_op jit(solution)/shard_map/ppermute | solution.py:115
  279.8 7.0 %collective-permute-done.2 = bf16[16,2048]{1,0:T(8,128)(2,1)S(1)} collective-permute-done((bf16[16,2048]{1,0:T(8,128)(2,1)S(1)}, bf16[16,2048]{1,0:T(8,128)(2,1)S(1)}, u32[]{:S(2)}, u32[]{:S(2)}) %collective-permute-start.2) | collective-permute-done | bytes 65568 | tf_op jit(solution)/shard_map/ppermute | solution.py:115
  286.8 7.0 %collective-permute-done.3 = bf16[16,2048]{1,0:T(8,128)(2,1)S(1)} collective-permute-done((bf16[16,2048]{1,0:T(8,128)(2,1)S(1)}, bf16[16,2048]{1,0:T(8,128)(2,1)S(1)}, u32[]{:S(2)}, u32[]{:S(2)}) %collective-permute-start.3) | collective-permute-done | bytes 65568 | tf_op jit(solution)/shard_map/ppermute | solution.py:115
  293.7 7.5 %collective-permute-done.4 = bf16[16,2048]{1,0:T(8,128)(2,1)S(1)} collective-permute-done((bf16[16,2048]{1,0:T(8,128)(2,1)S(1)}, bf16[16,2048]{1,0:T(8,128)(2,1)S(1)}, u32[]{:S(2)}, u32[]{:S(2)}) %collective-permute-start.4) | collective-permute-done | bytes 65568 | tf_op jit(solution)/shard_map/ppermute | solution.py:115
  301.2 7.0 %collective-permute-done.5 = bf16[16,2048]{1,0:T(8,128)(2,1)S(1)} collective-permute-done((bf16[16,2048]{1,0:T(8,128)(2,1)S(1)}, bf16[16,2048]{1,0:T(8,128)(2,1)S(1)}, u32[]{:S(2)}, u32[]{:S(2)}) %collective-permute-start.5) | collective-permute-done | bytes 65568 | tf_op jit(solution)/shard_map/ppermute | solution.py:115
  308.2 7.0 %collective-permute-done.6 = bf16[16,2048]{1,0:T(8,128)(2,1)S(1)} collective-permute-done((bf16[16,2048]{1,0:T(8,128)(2,1)S(1)}, bf16[16,2048]{1,0:T(8,128)(2,1)S(1)}, u32[]{:S(2)}, u32[]{:S(2)}) %collective-permute-start.6) | collective-permute-done | bytes 65568 | tf_op jit(solution)/shard_map/ppermute | solution.py:115
  (123 shorter events, 39.4 us)
Async XLA Ops:
  7.2 5.6 %copy-start.2 = (bf16[128,256]{1,0:T(8,128)(2,1)S(1)}, bf16[128,256]{1,0:T(8,128)(2,1)}, u32[]{:S(2)}) copy-start(bf16[128,256]{1,0:T(8,128)(2,1)} %param.14) | copy-start | bytes 196612
  7.2 145.8 %all-gather.2.cloned.1.call-start = ((), (), s32[]{:S(2)}) async-start(), calls=%async_computation.1 | async-start | bytes 4718592 | tf_op jit(solution)/shard_map/all_gather | solution.py:98
  19.7 6.5 %copy-start.3 = (s32[2]{0:T(128)S(1)}, s32[2]{0:T(128)}, u32[]{:S(2)}) copy-start(s32[2]{0:T(128)} %param.17) | copy-start | bytes 28
  77.3 186.7 %all-reduce.2.cloned.1.call-start = ((), (), s32[]{:S(2)}) async-start(), calls=%async_computation.2 | async-start | bytes 4194304 | tf_op jit(solution)/shard_map/psum | solution.py:105
  212.1 1.5 copy-start.4
  212.1 52.0 %copy-start.1 = (bf16[128,2048]{1,0:T(8,128)(2,1)S(1)}, bf16[128,2048]{1,0:T(8,128)(2,1)}, u32[]{:S(2)}) copy-start(bf16[128,2048]{1,0:T(8,128)(2,1)} %param.20) | copy-start | bytes 1572868
  265.2 51.2 %copy-start = (bf16[128,2048]{1,0:T(8,128)(2,1)}, bf16[128,2048]{1,0:T(8,128)(2,1)S(1)}, u32[]{:S(2)}) copy-start(bf16[128,2048]{1,0:T(8,128)(2,1)S(1)} %add_convert_fusion) | copy-start | bytes 1572868
  265.9 7.0 %collective-permute-start = (bf16[16,2048]{1,0:T(8,128)(2,1)S(1)}, bf16[16,2048]{1,0:T(8,128)(2,1)S(1)}, u32[]{:S(2)}, u32[]{:S(2)}) collective-permute-start(bf16[16,2048]{1,0:T(8,128)(2,1)S(1)} %broadcast_select_fusion), channel_id=1, source_target_pairs={{0,4},{4,8},{8,12},{12,16},{16,20},{20,24},{24,28},{28,0},{1,5},{5... | collective-permute-start | bytes 196616 | tf_op jit(solution)/shard_map/ppermute | solution.py:115
  272.8 7.0 %collective-permute-start.1 = (bf16[16,2048]{1,0:T(8,128)(2,1)S(1)}, bf16[16,2048]{1,0:T(8,128)(2,1)S(1)}, u32[]{:S(2)}, u32[]{:S(2)}) collective-permute-start(bf16[16,2048]{1,0:T(8,128)(2,1)S(1)} %collective-permute-done), channel_id=1, source_target_pairs={{0,4},{4,8},{8,12},{12,16},{16,20},{20,24},{24,28},{28,0},{1,5},{5... | collective-permute-start | bytes 196616 | tf_op jit(solution)/shard_map/ppermute | solution.py:115
  279.8 7.0 %collective-permute-start.2 = (bf16[16,2048]{1,0:T(8,128)(2,1)S(1)}, bf16[16,2048]{1,0:T(8,128)(2,1)S(1)}, u32[]{:S(2)}, u32[]{:S(2)}) collective-permute-start(bf16[16,2048]{1,0:T(8,128)(2,1)S(1)} %collective-permute-done.1), channel_id=1, source_target_pairs={{0,4},{4,8},{8,12},{12,16},{16,20},{20,24},{24,28},{28,0},{1,5},{5... | collective-permute-start | bytes 196616 | tf_op jit(solution)/shard_map/ppermute | solution.py:115
  286.8 7.0 %collective-permute-start.3 = (bf16[16,2048]{1,0:T(8,128)(2,1)S(1)}, bf16[16,2048]{1,0:T(8,128)(2,1)S(1)}, u32[]{:S(2)}, u32[]{:S(2)}) collective-permute-start(bf16[16,2048]{1,0:T(8,128)(2,1)S(1)} %collective-permute-done.2), channel_id=1, source_target_pairs={{0,4},{4,8},{8,12},{12,16},{16,20},{20,24},{24,28},{28,0},{1,5},{5... | collective-permute-start | bytes 196616 | tf_op jit(solution)/shard_map/ppermute | solution.py:115
  293.7 7.5 %collective-permute-start.4 = (bf16[16,2048]{1,0:T(8,128)(2,1)S(1)}, bf16[16,2048]{1,0:T(8,128)(2,1)S(1)}, u32[]{:S(2)}, u32[]{:S(2)}) collective-permute-start(bf16[16,2048]{1,0:T(8,128)(2,1)S(1)} %collective-permute-done.3), channel_id=1, source_target_pairs={{0,4},{4,8},{8,12},{12,16},{16,20},{20,24},{24,28},{28,0},{1,5},{5... | collective-permute-start | bytes 196616 | tf_op jit(solution)/shard_map/ppermute | solution.py:115
  301.2 7.0 %collective-permute-start.5 = (bf16[16,2048]{1,0:T(8,128)(2,1)S(1)}, bf16[16,2048]{1,0:T(8,128)(2,1)S(1)}, u32[]{:S(2)}, u32[]{:S(2)}) collective-permute-start(bf16[16,2048]{1,0:T(8,128)(2,1)S(1)} %collective-permute-done.4), channel_id=1, source_target_pairs={{0,4},{4,8},{8,12},{12,16},{16,20},{20,24},{24,28},{28,0},{1,5},{5... | collective-permute-start | bytes 196616 | tf_op jit(solution)/shard_map/ppermute | solution.py:115
  308.2 7.0 %collective-permute-start.6 = (bf16[16,2048]{1,0:T(8,128)(2,1)S(1)}, bf16[16,2048]{1,0:T(8,128)(2,1)S(1)}, u32[]{:S(2)}, u32[]{:S(2)}) collective-permute-start(bf16[16,2048]{1,0:T(8,128)(2,1)S(1)} %collective-permute-done.5), channel_id=1, source_target_pairs={{0,4},{4,8},{8,12},{12,16},{16,20},{20,24},{24,28},{28,0},{1,5},{5... | collective-permute-start | bytes 196616 | tf_op jit(solution)/shard_map/ppermute | solution.py:115
Sparse Core Ops, SparseCore 0:
  77.4 75.5 all-gather.1
  213.7 50.2 all-reduce.1
